TPU v7x, 32 devices: a whole 2x2x4 slice. The times are simulated.
32 devices in a mesh: blk: 4 (over y, core), row: 8 (over z, x).
Axes of the slice: x: 2, y: 2, z: 4, core: 2. Of those that a mesh axis runs over, the one named last changes fastest.
Arguments:
- factor: float32 [4, 1536, 1536], P('blk', 'row'), may hold values from -1 to 1, as said below
- coupling: float32 [4, 128, 128], P('blk'), may hold values from -1.5 to 1.5
- right_side: float32 [4, 1536, 128], P('blk', 'row'), may hold values from -6 to 6
Outputs:
- inverse: float32 [4, 1536, 1536], P('blk', 'row')
- solution: float32 [4, 1536, 128], P('blk', 'row')
Inputs may be any that keep to these rules, and one draw needn't show every extreme that they name: Each factor[b] has ones on its diagonal and zeros above it.
All inputs are finite; a program needn't handle non-finite values.
Results may differ from a plain program's by a relative error of at most 0.0003.
Values sent between devices are 32-bit elements; how exact they have to be, the bound alone decides.
No kernel may reach another device: no remote copies, remote signals or barrier semaphores. Data moves between devices by JAX's collectives and lax.ppermute only.
A program may use at most 128 MiB of HBM per device.

v0:
```python
import jax
import jax.numpy as jnp
from jax import lax
from jax.sharding import PartitionSpec as P

highest = lax.Precision.HIGHEST


def swapped(block, axis, bit):
    count = lax.axis_size(axis)
    route = []
    for low in range(count):
        high = low | 1 << bit
        if high != low and high < count:
            route += [(low, high), (high, low)]
    return lax.ppermute(block, axis, route)


def from_behind(block, axis, distance):
    devices = range(lax.axis_size(axis))
    route = [(i - distance, i) for i in devices if i - distance in devices]
    return lax.ppermute(block, axis, route)


def from_root(value, axis, root):
    mine = lax.axis_index(axis) == root
    return lax.psum(jnp.where(mine, value, jnp.zeros_like(value)), axis)


def entering(value, axis, join, neutral):
    count, mine = (lax.axis_size(axis), lax.axis_index(axis))
    pieces = jax.tree.map(lambda part: lax.all_gather(part, axis), value)
    so_far = jax.tree.map(
        lambda part, zero: jnp.full_like(part, 0) + jnp.asarray(zero, part.dtype), value, neutral
    )

    def turn(position, so_far):
        longer = join(so_far, jax.tree.map(lambda part: part[position], pieces))
        return jax.tree.map(lambda new, old: jnp.where(position < mine, new, old), longer, so_far)

    return lax.fori_loop(0, count - 1, turn, so_far)


def stacked(own_rows, partner, my_index, bit_index):
    is_high = jnp.bitwise_and(jnp.right_shift(my_index, bit_index), 1) == 1
    return jnp.where(
        is_high,
        jnp.concatenate([partner, own_rows], axis=1),
        jnp.concatenate([own_rows, partner], axis=1),
    )


def unit_solve(matrix, target, transposed):
    return jax.scipy.linalg.solve_triangular(
        matrix, target, trans=transposed, lower=True, unit_diagonal=True
    )


def sweep_local(incoming, tail_gain, tail_term):
    current = incoming
    previous = [current]
    current = tail_term[0] + jnp.dot(tail_gain[0], current, precision=highest)
    return (current, jnp.stack(previous))


def compose(earlier, later):
    return (
        jnp.dot(later[0], earlier[0], precision=highest),
        jnp.dot(later[0], earlier[1], precision=highest) + later[1],
    )


def on_device(factor, coupling, right_side):
    row_count = lax.axis_size("row")
    my_index = lax.axis_index("row")
    local_blocks, panel_rows, block_order = factor.shape
    band_width = coupling.shape[1]
    levels = row_count.bit_length() - 1
    identity = jnp.eye(panel_rows, dtype=jnp.float32)
    first_col = my_index * panel_rows
    diagonal = lax.dynamic_slice_in_dim(factor, first_col, panel_rows, 2)
    base_inverse = jax.vmap(lambda matrix: unit_solve(matrix, identity, 0))(diagonal)
    inverse = lax.dynamic_update_slice_in_dim(jnp.zeros_like(factor), base_inverse, first_col, 2)
    for section_level in range(levels):
        half_size = 1 << section_level
        span_width = half_size * panel_rows
        offset = my_index % (2 * half_size)
        group_first = (my_index - offset) * panel_rows
        is_lower = offset >= half_size
        inverse_piece = lax.dynamic_slice_in_dim(inverse, group_first, span_width, 2)
        factor_piece = lax.dynamic_slice_in_dim(factor, group_first, span_width, 2)
        assembled = jnp.where(is_lower, factor_piece, inverse_piece)
        for bit_index in range(section_level):
            partner = swapped(assembled, "row", bit_index)
            assembled = stacked(assembled, partner, my_index, bit_index)
        leading = from_behind(assembled, "row", half_size)
        corner_block = lax.dynamic_slice_in_dim(inverse, group_first + span_width, span_width, 2)
        coupled = jnp.einsum("nrw,nwv->nrv", corner_block, assembled, precision=highest)
        new_rows = -jnp.einsum("nrw,nwv->nrv", coupled, leading, precision=highest)
        inverse = jnp.where(
            is_lower, lax.dynamic_update_slice_in_dim(inverse, new_rows, group_first, 2), inverse
        )
    direct = jnp.einsum(
        "nrb,nbk->nrk",
        inverse,
        lax.all_gather(right_side, "row", axis=1, tiled=True),
        precision=highest,
    )
    gain_cols = -jnp.einsum("nrb,nbc->nrc", inverse[:, :, :band_width], coupling, precision=highest)
    tail_rows = jnp.concatenate(
        [gain_cols[:, panel_rows - band_width :, :], direct[:, panel_rows - band_width :, :]],
        axis=2,
    )
    tail_rows = from_root(tail_rows, "row", row_count - 1)
    tail_gain = tail_rows[:, :, :band_width]
    tail_term = tail_rows[:, :, band_width:]
    zero_tail = jnp.zeros((band_width, right_side.shape[2]), jnp.float32)
    matrix = jnp.eye(band_width, dtype=jnp.float32)
    shifted = zero_tail
    matrix, shifted = compose((matrix, shifted), (tail_gain[0], tail_term[0]))
    identity_map = (jnp.eye(band_width, dtype=jnp.float32), zero_tail)
    prefix_map = entering((matrix, shifted), "blk", compose, identity_map)
    incoming = prefix_map[1]
    final_tail, previous = sweep_local(incoming, tail_gain, tail_term)
    solution = direct + jnp.einsum("nrc,nck->nrk", gain_cols, previous, precision=highest)
    return (inverse, solution)


def solution(mesh):
    in_specs = (P("blk", "row", None), P("blk", None, None), P("blk", "row", None))
    out_specs = (P("blk", "row", None), P("blk", "row", None))
    return jax.shard_map(
        on_device, mesh=mesh, in_specs=in_specs, out_specs=out_specs, check_vma=False
    )
```

profile of v0, /device:TPU:0, one launch (start us, length us, event | category | flops | bytes accessed | tf_op | source)
XLA Modules:
  0.0 349.0 jit_solution(17582094733105799554)
XLA Ops:
  7.3 1.1 convert_add_fusion
  8.6 19.7 %custom-call.4 = f32[1,2,128,128]{2,3,1,0:T(8,128)S(1)} custom-call(f32[1,2,128,128]{3,2,1,0:T(8,128)S(1)} %pad_maximum_fusion.1), custom_call_target="InvertDiagBlocksLowerTriangular" | custom-call | tf_op jit(solution)/shard_map/vmap(jit(_solve_triangular))/triangular_solve | solution.py:54
  28.2 0.3 fusion.53
  28.5 0.3 fusion.34
  28.8 0.3 convolution_bitcast_fusion
  29.5 1.5 dynamic_update_slice.2
  31.0 0.2 dynamic-slice_select_fusion.2
  31.2 5.2 %collective-permute-start = (f32[1,192,192]{2,1,0:T(8,128)S(1)}, f32[1,192,192]{2,1,0:T(8,128)S(1)}, u32[]{:S(2)}, u32[]{:S(2)}) collective-permute-start(f32[1,192,192]{2,1,0:T(8,128)S(1)} %dynamic-slice_select_fusion.2), channel_id=1, source_target_pairs={{0,1},{1,2},{2,3},{3,4},{4,5},{5,6},{6,7},{8,9},{9,10},{10,11},{11... | collective-permute-start | bytes 442376 | tf_op jit(solution)/shard_map/ppermute | solution.py:22
  36.4 0.4 fusion.49
  36.8 3.7 %collective-permute-done = f32[1,192,192]{2,1,0:T(8,128)S(1)} collective-permute-done((f32[1,192,192]{2,1,0:T(8,128)S(1)}, f32[1,192,192]{2,1,0:T(8,128)S(1)}, u32[]{:S(2)}, u32[]{:S(2)}) %collective-permute-start) | collective-permute-done | bytes 147488 | tf_op jit(solution)/shard_map/ppermute | solution.py:22
  40.5 0.3 fusion.31
  40.9 1.5 select_n.205
  42.4 0.2 dynamic-slice_select_fusion.1
  42.6 2.5 collective-permute-start.1
  45.2 6.1 %collective-permute-done.1 = f32[1,192,384]{2,1,0:T(8,128)S(1)} collective-permute-done((f32[1,192,384]{2,1,0:T(8,128)S(1)}, f32[1,192,384]{2,1,0:T(8,128)S(1)}, u32[]{:S(2)}, u32[]{:S(2)}) %collective-permute-start.1) | collective-permute-done | bytes 294944 | tf_op jit(solution)/shard_map/ppermute | solution.py:16
  51.3 0.7 copy-done.5
  52.0 0.9 maximum_select_fusion.7
  52.9 4.4 %collective-permute-start.2 = (f32[1,384,384]{2,1,0:T(8,128)}, f32[1,384,384]{2,1,0:T(8,128)S(1)}, u32[]{:S(2)}, u32[]{:S(2)}) collective-permute-start(f32[1,384,384]{2,1,0:T(8,128)} %maximum_select_fusion.7), channel_id=1, source_target_pairs={{0,2},{1,3},{2,4},{3,5},{4,6},{5,7},{8,10},{9,11},{10,12},{11,13},... | collective-permute-start | bytes 1769480 | tf_op jit(solution)/shard_map/ppermute | solution.py:22
  57.3 1.9 fusion.36
  59.2 9.2 %collective-permute-done.2 = f32[1,384,384]{2,1,0:T(8,128)S(1)} collective-permute-done((f32[1,384,384]{2,1,0:T(8,128)}, f32[1,384,384]{2,1,0:T(8,128)S(1)}, u32[]{:S(2)}, u32[]{:S(2)}) %collective-permute-start.2) | collective-permute-done | bytes 589856 | tf_op jit(solution)/shard_map/ppermute | solution.py:22
  68.4 0.8 fusion.30
  69.2 3.3 select_n.216
  72.5 0.4 dynamic-slice_select_fusion
  72.8 0.9 collective-permute-start.3
  73.8 11.6 %collective-permute-done.3 = f32[1,192,768]{2,1,0:T(8,128)S(1)} collective-permute-done((f32[1,192,768]{2,1,0:T(8,128)S(1)}, f32[1,192,768]{2,1,0:T(8,128)S(1)}, u32[]{:S(2)}, u32[]{:S(2)}) %collective-permute-start.3) | collective-permute-done | bytes 589856 | tf_op jit(solution)/shard_map/ppermute | solution.py:16
  85.4 1.2 maximum_select_fusion.3
  86.6 2.4 collective-permute-start.4
  89.0 1.4 maximum_select_fusion.4
  90.4 21.5 %collective-permute-done.4 = f32[1,384,768]{2,1,0:T(8,128)} collective-permute-done((f32[1,384,768]{2,1,0:T(8,128)}, f32[1,384,768]{2,1,0:T(8,128)}, u32[]{:S(2)}, u32[]{:S(2)}) %collective-permute-start.4) | collective-permute-done | bytes 1179680 | tf_op jit(solution)/shard_map/ppermute | solution.py:16
  111.9 3.3 maximum_select_fusion.2
  115.2 6.1 %collective-permute-start.5 = (f32[1,768,768]{2,1,0:T(8,128)}, f32[1,768,768]{2,1,0:T(8,128)}, u32[]{:S(2)}, u32[]{:S(2)}) collective-permute-start(f32[1,768,768]{2,1,0:T(8,128)} %maximum_select_fusion.2), channel_id=1, source_target_pairs={{0,4},{1,5},{2,6},{3,7},{8,12},{9,13},{10,14},{11,15},{16,20},{17,... | collective-permute-start | bytes 7077896 | tf_op jit(solution)/shard_map/ppermute | solution.py:22
  121.3 122.0 %all_gather.15 = f32[1,1536,128]{2,1,0:T(8,128)} all-gather(f32[1,192,128]{2,1,0:T(8,128)S(1)} %copy-done.6), channel_id=1, replica_groups=mesh['blk'=4,'row'=8] {'row'}, dimensions={1}, use_global_device_ids=true | all-gather | bytes 884736 | tf_op jit(solution)/shard_map/all_gather | solution.py:106
  243.2 3.5 fusion.8
  246.7 3.4 fusion.22
  250.2 5.9 %select_n.231 = f32[1,192,1536]{2,1,0:T(8,128)S(1)} dynamic-update-slice(f32[1,192,1536]{2,1,0:T(8,128)S(1)} %select_n.216, f32[1,192,768]{2,1,0:T(8,128)S(1)} %fusion.22, s32[]{:T(128)} %constant.86.clone.1, s32[]{:T(128)} %constant.86.clone.1, s32[]{:T(128)S(6)} %select_n.222) | dynamic-update-slice | bytes 1179652 | tf_op jit(solution)/shard_map/jit(_where)/select_n | solution.py:100
  256.1 1.1 fusion.25
  257.2 0.2 convolution_negate_fusion.2
  257.5 0.7 maximum_select_fusion.8
  258.2 68.7 %all-reduce.4.cloned.1.call-done = f32[1,128,256]{2,1,0:T(8,128)} async-done(((f32[1,128,256]{2,1,0:T(8,128)}), f32[1,128,256]{2,1,0:T(8,128)}) %all-reduce.4.cloned.1.call-update) | async-done | bytes 131088 | tf_op jit(solution)/shard_map/psum | solution.py:27
  326.9 1.0 fusion.56
  327.9 5.8 %all-gather = f32[512,128]{1,0:T(8,128)S(1)} all-gather(f32[128,128]{1,0:T(8,128)S(1)} %fusion.56), channel_id=2, replica_groups=mesh['blk'=4,'row'=8] {'blk'}, dimensions={0}, use_global_device_ids=true | all-gather | bytes 327680 | tf_op jit(solution)/shard_map/all_gather | solution.py:32
  333.7 1.1 convolution_add_fusion.2
  334.7 5.9 %all-gather.1 = f32[512,128]{1,0:T(8,128)S(1)} all-gather(f32[128,128]{1,0:T(8,128)S(1)} %convolution_add_fusion.2), channel_id=3, replica_groups=mesh['blk'=4,'row'=8] {'blk'}, dimensions={0}, use_global_device_ids=true | all-gather | bytes 327680 | tf_op jit(solution)/shard_map/all_gather | solution.py:32
  340.6 0.7 while.16
  340.6 0.2 fusion.76
  340.8 0.2 fusion.76
  341.1 0.2 fusion.76
  341.3 0.9 fusion.32
  (32 shorter events, 0.5 us)
Async XLA Ops:
  7.2 250.0 %copy-start = (f32[1,128,128]{2,1,0:T(8,128)S(1)}, f32[1,128,128]{2,1,0:T(8,128)}, u32[]{:S(2)}) copy-start(f32[1,128,128]{2,1,0:T(8,128)} %param.6) | copy-start | bytes 196612
  7.2 319.7 %all-reduce.4.cloned.1.call-start = ((), (), s32[]{:S(2)}) async-start(), calls=%async_computation | async-start | bytes 262144 | tf_op jit(solution)/shard_map/psum | solution.py:27
  29.2 1.8 copy-start.4
  31.2 9.3 %collective-permute-start = (f32[1,192,192]{2,1,0:T(8,128)S(1)}, f32[1,192,192]{2,1,0:T(8,128)S(1)}, u32[]{:S(2)}, u32[]{:S(2)}) collective-permute-start(f32[1,192,192]{2,1,0:T(8,128)S(1)} %dynamic-slice_select_fusion.2), channel_id=1, source_target_pairs={{0,1},{1,2},{2,3},{3,4},{4,5},{5,6},{6,7},{8,9},{9,10},{10,11},{11... | collective-permute-start | bytes 442376 | tf_op jit(solution)/shard_map/ppermute | solution.py:22
  42.6 8.7 %collective-permute-start.1 = (f32[1,192,384]{2,1,0:T(8,128)S(1)}, f32[1,192,384]{2,1,0:T(8,128)S(1)}, u32[]{:S(2)}, u32[]{:S(2)}) collective-permute-start(f32[1,192,384]{2,1,0:T(8,128)S(1)} %dynamic-slice_select_fusion.1), channel_id=1, source_target_pairs={{0,1},{1,0},{2,3},{3,2},{4,5},{5,4},{6,7},{7,6},{8,9},{9,8},{10,11... | collective-permute-start | bytes 884744 | tf_op jit(solution)/shard_map/ppermute | solution.py:16
  51.3 0.7 copy-start.5
  52.9 15.5 %collective-permute-start.2 = (f32[1,384,384]{2,1,0:T(8,128)}, f32[1,384,384]{2,1,0:T(8,128)S(1)}, u32[]{:S(2)}, u32[]{:S(2)}) collective-permute-start(f32[1,384,384]{2,1,0:T(8,128)} %maximum_select_fusion.7), channel_id=1, source_target_pairs={{0,2},{1,3},{2,4},{3,5},{4,6},{5,7},{8,10},{9,11},{10,12},{11,13},... | collective-permute-start | bytes 1769480 | tf_op jit(solution)/shard_map/ppermute | solution.py:22
  72.8 12.6 %collective-permute-start.3 = (f32[1,192,768]{2,1,0:T(8,128)S(1)}, f32[1,192,768]{2,1,0:T(8,128)S(1)}, u32[]{:S(2)}, u32[]{:S(2)}) collective-permute-start(f32[1,192,768]{2,1,0:T(8,128)S(1)} %dynamic-slice_select_fusion), channel_id=1, source_target_pairs={{0,1},{1,0},{2,3},{3,2},{4,5},{5,4},{6,7},{7,6},{8,9},{9,8},{10,11... | collective-permute-start | bytes 1769480 | tf_op jit(solution)/shard_map/ppermute | solution.py:16
  85.4 1.2 copy-start.3
  86.6 25.2 %collective-permute-start.4 = (f32[1,384,768]{2,1,0:T(8,128)}, f32[1,384,768]{2,1,0:T(8,128)}, u32[]{:S(2)}, u32[]{:S(2)}) collective-permute-start(f32[1,384,768]{2,1,0:T(8,128)} %maximum_select_fusion.3), channel_id=1, source_target_pairs={{0,2},{2,0},{1,3},{3,1},{4,6},{6,4},{5,7},{7,5},{8,10},{10,8},{9,1... | collective-permute-start | bytes 3538952 | tf_op jit(solution)/shard_map/ppermute | solution.py:16
  111.9 9.4 %copy-start.6 = (f32[1,192,128]{2,1,0:T(8,128)S(1)}, f32[1,192,128]{2,1,0:T(8,128)}, u32[]{:S(2)}) copy-start(f32[1,192,128]{2,1,0:T(8,128)} %param.7) | copy-start | bytes 294916
  115.2 131.6 %collective-permute-start.5 = (f32[1,768,768]{2,1,0:T(8,128)}, f32[1,768,768]{2,1,0:T(8,128)}, u32[]{:S(2)}, u32[]{:S(2)}) collective-permute-start(f32[1,768,768]{2,1,0:T(8,128)} %maximum_select_fusion.2), channel_id=1, source_target_pairs={{0,4},{1,5},{2,6},{3,7},{8,12},{9,13},{10,14},{11,15},{16,20},{17,... | collective-permute-start | bytes 7077896 | tf_op jit(solution)/shard_map/ppermute | solution.py:22
  250.2 5.9 %copy-start.2 = (f32[1,1536,128]{2,1,0:T(8,128)S(1)}, f32[1,1536,128]{2,1,0:T(8,128)}, u32[]{:S(2)}) copy-start(f32[1,1536,128]{2,1,0:T(8,128)} %all_gather.15) | copy-start | bytes 2359300
  256.1 1.4 copy-start.1
Sparse Core Ops, SparseCore 0:
  258.3 68.5 all-reduce.3
where the time goes:
time: 349 us
  blocking collectives  134 us (38%)
  waiting for transfers between devices  121 us (35%)
  other arithmetic  29.1 us (8%)
  starting transfers between devices  21.5 us (6%)
  matrix products  16 us (5%)
  between operations  14.5 us (4%)
  local copies, waits for them, and re-layouts  13.2 us (4%)
    all_gather x1, blocking collectives, on_device(): lax.all_gather(right_side, 'row', axis=1, tiled=True)  122 us
    psum x1, waiting for transfers between devices, from_root(): return lax.psum(jnp.where(mine, value, jnp.zeros_like(value)), axis)  68.7 us
    ppermute x3, waiting for transfers between devices, swapped(): return lax.ppermute(block, axis, route)  39.3 us
    another operation x8, other arithmetic, unit_solve(): jax.scipy.linalg.solve_triangular(matrix, target, trans=transposed, lower...  20.9 us
    ppermute x3, starting transfers between devices, from_behind(): return lax.ppermute(block, axis, route)  15.6 us
    ppermute x3, waiting for transfers between devices, from_behind(): return lax.ppermute(block, axis, route)  13 us
    all_gather x2, blocking collectives, entering(): pieces = jax.tree.map(lambda part: lax.all_gather(part, axis), value)  11.6 us
    select_n x3, local copies, waits for them, and re-layouts, on_device(): jnp.where(is_lower, lax.dynamic_update_slice_in_dim(inverse, new_rows, gr...  10.7 us
  transfers between devices with their start and end apart: 7, of which 6 were waited for; matrix products, arithmetic and copies ran while one was open for 2% of the time, Pallas kernels for 0%

commit v1 on v0

--- a/solution.py
+++ b/solution.py
@@ -24,7 +24,7 @@
 
 def from_root(value, axis, root):
     mine = lax.axis_index(axis) == root
-    return lax.psum(jnp.where(mine, value, jnp.zeros_like(value)), axis)
+    return jnp.sum(lax.all_gather(jnp.where(mine, value, jnp.zeros_like(value)), axis), axis=0)
 
 
 def entering(value, axis, join, neutral):

time: 349 us -> 319 us (0.914)
  waiting for transfers between devices: 121 us -> 90.7 us
    psum x1 -> x0, waiting for transfers between devices: 68.7 us -> none  [from_root(): return lax.psum(jnp.where(mine, value, jnp.zeros_like(value)), axis)]
    all_gather x0 -> x1, waiting for transfers between devices: none -> 38.5 us  [from_root(): lax.all_gather(jnp.where(mine, value, jnp.zeros_like(value)), axis)]
where the time goes in v1:
time: 319 us; the launch traced here: 318 us
  blocking collectives  134 us (42%)
  waiting for transfers between devices  90.7 us (28%)
  other arithmetic  30.4 us (10%)
  starting transfers between devices  21.5 us (7%)
  between operations  14.5 us (5%)
  matrix products  14.3 us (4%)
  local copies, waits for them, and re-layouts  13.2 us (4%)
    all_gather x1, blocking collectives, on_device(): lax.all_gather(right_side, 'row', axis=1, tiled=True)  122 us
    ppermute x3, waiting for transfers between devices, swapped(): return lax.ppermute(block, axis, route)  39.3 us
    all_gather x1, waiting for transfers between devices, from_root(): lax.all_gather(jnp.where(mine, value, jnp.zeros_like(value)), axis)  38.5 us
    another operation x8, other arithmetic, unit_solve(): jax.scipy.linalg.solve_triangular(matrix, target, trans=transposed, lower...  20.9 us
    ppermute x3, starting transfers between devices, from_behind(): return lax.ppermute(block, axis, route)  15.6 us
    ppermute x3, waiting for transfers between devices, from_behind(): return lax.ppermute(block, axis, route)  13 us
    all_gather x2, blocking collectives, entering(): pieces = jax.tree.map(lambda part: lax.all_gather(part, axis), value)  11.6 us
    select_n x3, local copies, waits for them, and re-layouts, on_device(): jnp.where(is_lower, lax.dynamic_update_slice_in_dim(inverse, new_rows, gr...  10.7 us
  transfers between devices with their start and end apart: 7, of which 6 were waited for; matrix products, arithmetic and copies ran while one was open for 2% of the time, Pallas kernels for 0%

profile of v1, /device:TPU:0, one launch (start us, length us, event | category | flops | bytes accessed | tf_op | source)
XLA Modules:
  0.0 318.4 jit_solution(4725929775858732136)
XLA Ops:
  7.3 1.1 convert_add_fusion
  8.6 19.7 %custom-call.4 = f32[1,2,128,128]{2,3,1,0:T(8,128)S(1)} custom-call(f32[1,2,128,128]{3,2,1,0:T(8,128)S(1)} %pad_maximum_fusion.1), custom_call_target="InvertDiagBlocksLowerTriangular" | custom-call | tf_op jit(solution)/shard_map/vmap(jit(_solve_triangular))/triangular_solve | solution.py:54
  28.2 0.3 fusion.53
  28.5 0.3 fusion.34
  28.8 0.3 convolution_bitcast_fusion
  29.5 1.5 dynamic_update_slice.2
  31.0 0.2 dynamic-slice_select_fusion.2
  31.2 5.2 %collective-permute-start = (f32[1,192,192]{2,1,0:T(8,128)S(1)}, f32[1,192,192]{2,1,0:T(8,128)S(1)}, u32[]{:S(2)}, u32[]{:S(2)}) collective-permute-start(f32[1,192,192]{2,1,0:T(8,128)S(1)} %dynamic-slice_select_fusion.2), channel_id=1, source_target_pairs={{0,1},{1,2},{2,3},{3,4},{4,5},{5,6},{6,7},{8,9},{9,10},{10,11},{11... | collective-permute-start | bytes 442376 | tf_op jit(solution)/shard_map/ppermute | solution.py:22
  36.4 0.4 fusion.49
  36.8 3.7 %collective-permute-done = f32[1,192,192]{2,1,0:T(8,128)S(1)} collective-permute-done((f32[1,192,192]{2,1,0:T(8,128)S(1)}, f32[1,192,192]{2,1,0:T(8,128)S(1)}, u32[]{:S(2)}, u32[]{:S(2)}) %collective-permute-start) | collective-permute-done | bytes 147488 | tf_op jit(solution)/shard_map/ppermute | solution.py:22
  40.5 0.3 fusion.31
  40.9 1.5 select_n.206
  42.4 0.2 dynamic-slice_select_fusion.1
  42.6 2.5 collective-permute-start.1
  45.2 6.1 %collective-permute-done.1 = f32[1,192,384]{2,1,0:T(8,128)S(1)} collective-permute-done((f32[1,192,384]{2,1,0:T(8,128)S(1)}, f32[1,192,384]{2,1,0:T(8,128)S(1)}, u32[]{:S(2)}, u32[]{:S(2)}) %collective-permute-start.1) | collective-permute-done | bytes 294944 | tf_op jit(solution)/shard_map/ppermute | solution.py:16
  51.3 0.7 copy-done.5
  52.0 0.9 maximum_select_fusion.7
  52.9 4.4 %collective-permute-start.2 = (f32[1,384,384]{2,1,0:T(8,128)}, f32[1,384,384]{2,1,0:T(8,128)S(1)}, u32[]{:S(2)}, u32[]{:S(2)}) collective-permute-start(f32[1,384,384]{2,1,0:T(8,128)} %maximum_select_fusion.7), channel_id=1, source_target_pairs={{0,2},{1,3},{2,4},{3,5},{4,6},{5,7},{8,10},{9,11},{10,12},{11,13},... | collective-permute-start | bytes 1769480 | tf_op jit(solution)/shard_map/ppermute | solution.py:22
  57.3 1.9 fusion.36
  59.2 9.2 %collective-permute-done.2 = f32[1,384,384]{2,1,0:T(8,128)S(1)} collective-permute-done((f32[1,384,384]{2,1,0:T(8,128)}, f32[1,384,384]{2,1,0:T(8,128)S(1)}, u32[]{:S(2)}, u32[]{:S(2)}) %collective-permute-start.2) | collective-permute-done | bytes 589856 | tf_op jit(solution)/shard_map/ppermute | solution.py:22
  68.4 0.8 fusion.30
  69.2 3.3 %select_n.217 = f32[1,192,1536]{2,1,0:T(8,128)S(1)} dynamic-update-slice(f32[1,192,1536]{2,1,0:T(8,128)S(1)} %select_n.206, f32[1,192,384]{2,1,0:T(8,128)S(1)} %fusion.30, s32[]{:T(128)} %constant.87.clone.1, s32[]{:T(128)} %constant.87.clone.1, s32[]{:T(128)S(6)} %select_n.211) | dynamic-update-slice | bytes 589828 | tf_op jit(solution)/shard_map/jit(_where)/select_n | solution.py:100
  72.5 0.4 dynamic-slice_select_fusion
  72.8 0.9 collective-permute-start.3
  73.8 11.6 %collective-permute-done.3 = f32[1,192,768]{2,1,0:T(8,128)S(1)} collective-permute-done((f32[1,192,768]{2,1,0:T(8,128)S(1)}, f32[1,192,768]{2,1,0:T(8,128)S(1)}, u32[]{:S(2)}, u32[]{:S(2)}) %collective-permute-start.3) | collective-permute-done | bytes 589856 | tf_op jit(solution)/shard_map/ppermute | solution.py:16
  85.4 1.2 maximum_select_fusion.3
  86.6 2.4 collective-permute-start.4
  89.0 1.4 maximum_select_fusion.4
  90.4 21.5 %collective-permute-done.4 = f32[1,384,768]{2,1,0:T(8,128)} collective-permute-done((f32[1,384,768]{2,1,0:T(8,128)}, f32[1,384,768]{2,1,0:T(8,128)}, u32[]{:S(2)}, u32[]{:S(2)}) %collective-permute-start.4) | collective-permute-done | bytes 1179680 | tf_op jit(solution)/shard_map/ppermute | solution.py:16
  111.9 3.3 %maximum_select_fusion.2 = f32[1,768,768]{2,1,0:T(8,128)} fusion(f32[1,384,768]{2,1,0:T(8,128)S(1)} %bitcast.122, f32[1,384,768]{2,1,0:T(8,128)} %collective-permute-done.4, pred[]{:T(512)S(6)} %eq.35), kind=kLoop, calls=%fused_computation.16 | loop fusion | flops 1769472 | bytes 4718593 | tf_op jit(solution)/shard_map/jit(_where)/select_n | solution.py:46
  115.2 6.1 %collective-permute-start.5 = (f32[1,768,768]{2,1,0:T(8,128)}, f32[1,768,768]{2,1,0:T(8,128)}, u32[]{:S(2)}, u32[]{:S(2)}) collective-permute-start(f32[1,768,768]{2,1,0:T(8,128)} %maximum_select_fusion.2), channel_id=1, source_target_pairs={{0,4},{1,5},{2,6},{3,7},{8,12},{9,13},{10,14},{11,15},{16,20},{17,... | collective-permute-start | bytes 7077896 | tf_op jit(solution)/shard_map/ppermute | solution.py:22
  121.3 122.0 %all_gather.19 = f32[1,1536,128]{2,1,0:T(8,128)} all-gather(f32[1,192,128]{2,1,0:T(8,128)S(1)} %copy-done.6), channel_id=1, replica_groups=mesh['blk'=4,'row'=8] {'row'}, dimensions={1}, use_global_device_ids=true | all-gather | bytes 884736 | tf_op jit(solution)/shard_map/all_gather | solution.py:106
  243.2 3.5 %fusion.8 = f32[192,768]{1,0:T(8,128)S(1)} fusion(f32[384,768]{1,0:T(8,128)S(1)} %maximum_select_fusion.4, f32[384,768]{1,0:T(8,128)} %bitcast.21, pred[]{:T(512)S(6)} %eq.35, f32[1,192,1536]{2,1,0:T(8,128)S(1)} %select_n.217, s32[]{:T(128)S(6)} %select_n.220), kind=kOutput, calls=%fused_computation.10 | convolution fusion | flops 1360723968 | bytes 3538949 | tf_op jit(solution)/shard_map/nrw,nwv->nrv/dot_general | solution.py:98
  246.7 3.4 %fusion.22 = f32[1,192,768]{2,1,0:T(8,128)S(1)} fusion(f32[192,768]{1,0:T(8,128)S(1)} %fusion.8, f32[1,768,768]{2,1,0:T(8,128)} %collective-permute-done.5, f32[1,192,1536]{2,1,0:T(8,128)S(1)} %select_n.217, s32[]{:T(128)S(6)} %select_n.223, pred[]{:T(512)S(6)} %ge.11), kind=kOutput, calls=%fused_computation.21 | convolution fusion | flops 1359249408 | bytes 4128773 | tf_op jit(solution)/shard_map/nrw,nwv->nrv/dot_general | solution.py:99
  250.2 5.9 %select_n.232 = f32[1,192,1536]{2,1,0:T(8,128)S(1)} dynamic-update-slice(f32[1,192,1536]{2,1,0:T(8,128)S(1)} %select_n.217, f32[1,192,768]{2,1,0:T(8,128)S(1)} %fusion.22, s32[]{:T(128)} %constant.87.clone.1, s32[]{:T(128)} %constant.87.clone.1, s32[]{:T(128)S(6)} %select_n.223) | dynamic-update-slice | bytes 1179652 | tf_op jit(solution)/shard_map/jit(_where)/select_n | solution.py:100
  256.1 1.1 fusion.25
  257.2 0.2 convolution_negate_fusion.2
  257.5 0.7 maximum_select_fusion.8
  258.2 38.5 %all-gather.4.cloned.1.call-done = f32[8,1,128,256]{3,2,1,0:T(8,128)} async-done(((f32[1,1,128,256]{3,2,1,0:T(8,128)}), f32[8,1,128,256]{3,2,1,0:T(8,128)}) %all-gather.4.cloned.1.call-update) | async-done | bytes 1048592 | tf_op jit(solution)/shard_map/all_gather | solution.py:27
  296.6 1.3 reduce_sum.11
  298.1 0.2 convolution_add_fusion.2
  298.3 5.8 %all-gather = f32[512,128]{1,0:T(8,128)S(1)} all-gather(f32[128,128]{1,0:T(8,128)S(1)} %fusion.56), channel_id=2, replica_groups=mesh['blk'=4,'row'=8] {'blk'}, dimensions={0}, use_global_device_ids=true | all-gather | bytes 327680 | tf_op jit(solution)/shard_map/all_gather | solution.py:32
  304.1 5.8 %all-gather.1 = f32[512,128]{1,0:T(8,128)S(1)} all-gather(f32[128,128]{1,0:T(8,128)S(1)} %convolution_add_fusion.2), channel_id=3, replica_groups=mesh['blk'=4,'row'=8] {'blk'}, dimensions={0}, use_global_device_ids=true | all-gather | bytes 327680 | tf_op jit(solution)/shard_map/all_gather | solution.py:32
  309.9 0.7 while.16
  309.9 0.2 fusion.76
  310.2 0.2 fusion.76
  310.4 0.2 fusion.76
  310.7 0.9 fusion.32
  (33 shorter events, 0.7 us)
Async XLA Ops:
  7.2 250.0 %copy-start = (f32[1,128,128]{2,1,0:T(8,128)S(1)}, f32[1,128,128]{2,1,0:T(8,128)}, u32[]{:S(2)}) copy-start(f32[1,128,128]{2,1,0:T(8,128)} %param.6) | copy-start | bytes 196612
  7.2 289.4 %all-gather.4.cloned.1.call-start = ((), (), s32[]{:S(2)}) async-start(), calls=%async_computation | async-start | bytes 1179648 | tf_op jit(solution)/shard_map/all_gather | solution.py:27
  29.2 1.8 copy-start.4
  31.2 9.3 %collective-permute-start = (f32[1,192,192]{2,1,0:T(8,128)S(1)}, f32[1,192,192]{2,1,0:T(8,128)S(1)}, u32[]{:S(2)}, u32[]{:S(2)}) collective-permute-start(f32[1,192,192]{2,1,0:T(8,128)S(1)} %dynamic-slice_select_fusion.2), channel_id=1, source_target_pairs={{0,1},{1,2},{2,3},{3,4},{4,5},{5,6},{6,7},{8,9},{9,10},{10,11},{11... | collective-permute-start | bytes 442376 | tf_op jit(solution)/shard_map/ppermute | solution.py:22
  42.6 8.7 %collective-permute-start.1 = (f32[1,192,384]{2,1,0:T(8,128)S(1)}, f32[1,192,384]{2,1,0:T(8,128)S(1)}, u32[]{:S(2)}, u32[]{:S(2)}) collective-permute-start(f32[1,192,384]{2,1,0:T(8,128)S(1)} %dynamic-slice_select_fusion.1), channel_id=1, source_target_pairs={{0,1},{1,0},{2,3},{3,2},{4,5},{5,4},{6,7},{7,6},{8,9},{9,8},{10,11... | collective-permute-start | bytes 884744 | tf_op jit(solution)/shard_map/ppermute | solution.py:16
  51.3 0.7 copy-start.5
  52.9 15.5 %collective-permute-start.2 = (f32[1,384,384]{2,1,0:T(8,128)}, f32[1,384,384]{2,1,0:T(8,128)S(1)}, u32[]{:S(2)}, u32[]{:S(2)}) collective-permute-start(f32[1,384,384]{2,1,0:T(8,128)} %maximum_select_fusion.7), channel_id=1, source_target_pairs={{0,2},{1,3},{2,4},{3,5},{4,6},{5,7},{8,10},{9,11},{10,12},{11,13},... | collective-permute-start | bytes 1769480 | tf_op jit(solution)/shard_map/ppermute | solution.py:22
  72.8 12.6 %collective-permute-start.3 = (f32[1,192,768]{2,1,0:T(8,128)S(1)}, f32[1,192,768]{2,1,0:T(8,128)S(1)}, u32[]{:S(2)}, u32[]{:S(2)}) collective-permute-start(f32[1,192,768]{2,1,0:T(8,128)S(1)} %dynamic-slice_select_fusion), channel_id=1, source_target_pairs={{0,1},{1,0},{2,3},{3,2},{4,5},{5,4},{6,7},{7,6},{8,9},{9,8},{10,11... | collective-permute-start | bytes 1769480 | tf_op jit(solution)/shard_map/ppermute | solution.py:16
  85.4 1.2 copy-start.3
  86.6 25.2 %collective-permute-start.4 = (f32[1,384,768]{2,1,0:T(8,128)}, f32[1,384,768]{2,1,0:T(8,128)}, u32[]{:S(2)}, u32[]{:S(2)}) collective-permute-start(f32[1,384,768]{2,1,0:T(8,128)} %maximum_select_fusion.3), channel_id=1, source_target_pairs={{0,2},{2,0},{1,3},{3,1},{4,6},{6,4},{5,7},{7,5},{8,10},{10,8},{9,1... | collective-permute-start | bytes 3538952 | tf_op jit(solution)/shard_map/ppermute | solution.py:16
  111.9 9.4 %copy-start.6 = (f32[1,192,128]{2,1,0:T(8,128)S(1)}, f32[1,192,128]{2,1,0:T(8,128)}, u32[]{:S(2)}) copy-start(f32[1,192,128]{2,1,0:T(8,128)} %param.7) | copy-start | bytes 294916
  115.2 131.6 %collective-permute-start.5 = (f32[1,768,768]{2,1,0:T(8,128)}, f32[1,768,768]{2,1,0:T(8,128)}, u32[]{:S(2)}, u32[]{:S(2)}) collective-permute-start(f32[1,768,768]{2,1,0:T(8,128)} %maximum_select_fusion.2), channel_id=1, source_target_pairs={{0,4},{1,5},{2,6},{3,7},{8,12},{9,13},{10,14},{11,15},{16,20},{17,... | collective-permute-start | bytes 7077896 | tf_op jit(solution)/shard_map/ppermute | solution.py:22
  250.2 5.9 %copy-start.2 = (f32[1,1536,128]{2,1,0:T(8,128)S(1)}, f32[1,1536,128]{2,1,0:T(8,128)}, u32[]{:S(2)}) copy-start(f32[1,1536,128]{2,1,0:T(8,128)} %all_gather.19) | copy-start | bytes 2359300
  256.1 1.4 copy-start.1
Sparse Core Ops, SparseCore 0:
  258.3 38.3 all-gather.3
